TPU v7x, 32 devices: a whole 2x2x4 slice. The times are simulated.
32 devices in a mesh: expert: 4 (over y, core), shard: 8 (over z, x).
Axes of the slice: x: 2, y: 2, z: 4, core: 2. Of those that a mesh axis runs over, the one named last changes fastest.
Arguments:
- train_down: float32 [16, 6400, 4096], P('expert', None, 'shard'), may hold values from -0.109375 to 0.109375
- other_down: bfloat16 [16, 6400, 4096], P('expert', None, 'shard'), may hold values from -0.0390625 to 0.0390625
- router_weight: float32 [4096, 16], P('shard', 'expert'), may hold values from -0.09375 to 0.09375
- router_gain: float32 [4096], P('shard'), may hold values from 0.25 to 1.75
Outputs:
- ready_down: bfloat16 [16, 6400, 4096], P('expert', 'shard')
- scale_down: float32 [16, 6400], P('expert', 'shard')
- serve_router: bfloat16 [4096, 16], replicated
All inputs are finite; a program needn't handle non-finite values.
Results may differ from a plain program's by a relative error of at most 0.001.
Values may be sent and summed in bfloat16 or wider, within the bound.
A program may use at most 256 MiB of HBM per device.

v0:
```python
import jax
import jax.numpy as jnp
from jax import lax
from jax.sharding import PartitionSpec as P


def per_device(train_down, other_down, router_weight, router_gain):
    latest_down = train_down + other_down.astype(jnp.float32)
    total_down = lax.psum(jnp.sum(latest_down * latest_down, axis=2), "shard")
    scale_down = jnp.sqrt(total_down)
    narrow_down = (latest_down / jnp.expand_dims(scale_down, 2)).astype(jnp.bfloat16)
    ready_down = lax.all_to_all(narrow_down, "shard", split_axis=1, concat_axis=2, tiled=True)
    scale_down = lax.dynamic_slice_in_dim(
        scale_down, lax.axis_index("shard") * ready_down.shape[1], ready_down.shape[1], axis=1
    )
    part_router = (router_weight * router_gain[:, None]).astype(jnp.bfloat16)
    row_router = lax.all_gather(part_router, "shard", axis=0, tiled=True)
    serve_router = lax.all_gather(row_router, "expert", axis=1, tiled=True)
    return (ready_down, scale_down, serve_router)


def solution(mesh):
    in_specs = (
        P("expert", None, "shard"),
        P("expert", None, "shard"),
        P("shard", "expert"),
        P("shard"),
    )
    out_specs = (P("expert", "shard", None), P("expert", "shard"), P())
    return jax.shard_map(
        per_device, mesh=mesh, in_specs=in_specs, out_specs=out_specs, check_vma=False
    )
```

profile of v0, /device:TPU:0, one launch (start us, length us, event | category | flops | bytes accessed | tf_op | source)
XLA Modules:
  0.0 905.5 jit_solution(8188198296431997854)
XLA Ops:
  7.2 0.0 all-reduce.2.cloned.1.call-start
  7.2 24.2 %multiply_reduce_fusion = f32[4,6400]{1,0:T(4,128)S(1)} fusion(f32[4,6400,512]{2,1,0:T(8,128)} %param.4, bf16[4,6400,512]{2,1,0:T(8,128)(2,1)} %param.5), kind=kLoop, calls=%fused_computation.1 | loop fusion | flops 52403200 | bytes 78745600 | tf_op jit(solution)/shard_map/reduce_sum | solution.py:9
  31.4 2.3 copy.21
  33.7 0.0 all-reduce.2.cloned.1.call-update
  33.7 135.6 %all-reduce.2.cloned.1.call-done = f32[4,6400]{0,1:T(8,128)} async-done(((f32[4,6400]{0,1:T(8,128)}), f32[4,6400]{0,1:T(8,128)}) %all-reduce.2.cloned.1.call-update) | async-done | bytes 102416 | tf_op jit(solution)/shard_map/psum | solution.py:9
  169.3 2.7 sqrt.3
  172.0 1.2 copy.17
  173.3 34.3 %divide_convert_fusion = bf16[4,6400,512]{2,1,0:T(8,128)(2,1)} fusion(f32[4,6400,512]{2,1,0:T(8,128)} %param.4, bf16[4,6400,512]{2,1,0:T(8,128)(2,1)} %param.5, f32[4,6400]{1,0:T(4,128)S(1)} %copy.17), kind=kLoop, calls=%fused_computation | loop fusion | flops 52428800 | bytes 104960000 | tf_op jit(solution)/shard_map/convert_element_type | solution.py:11
  207.5 33.4 %copy.18 = bf16[4,6400,512]{2,0,1:T(4,128)(2,1)} copy(bf16[4,6400,512]{2,1,0:T(8,128)(2,1)} %divide_convert_fusion) | data formatting | bytes 52428800 | tf_op jit(solution)/shard_map/convert_element_type | solution.py:11
  240.9 0.0 copy-start
  240.9 0.0 copy-start.1
  240.9 6.6 all-to-all-start
  247.6 0.0 copy-done
  247.6 0.0 copy-done.1
  247.6 585.0 %all_gather.6 = bf16[4096,4]{0,1:T(4,128)(2,1)S(1)} all-gather(bf16[512,4]{0,1:T(4,128)(2,1)S(1)} %multiply_convert_fusion), channel_id=1, replica_groups=mesh['expert'=4,'shard'=8] {'shard'}, dimensions={0}, use_global_device_ids=true | all-gather | bytes 36864 | tf_op jit(solution)/shard_map/all_gather | solution.py:17
  832.7 5.4 all-gather
  838.1 0.7 reshape.9
  838.8 0.8 constant_dynamic-slice_fusion
  839.5 1.8 copy.20
  841.3 0.0 all-to-all-done
  841.3 18.2 %copy.19 = bf16[4,800,8,512]{3,2,1,0:T(8,128)(2,1)} copy(bf16[4,800,8,512]{3,0,1,2:T(4,128)(2,1)} %bitcast.1) | data formatting | bytes 52428800 | tf_op jit(solution)/shard_map/all_to_all | solution.py:12
  859.5 39.2 %all_to_all.16 = bf16[4,800,4096]{2,1,0:T(8,128)(2,1)} reshape(bf16[4,800,8,512]{3,2,1,0:T(8,128)(2,1)} %copy.19) | data formatting | bytes 52428800 | tf_op jit(solution)/shard_map/all_to_all | solution.py:12
  (1 shorter events, 0.0 us)
Async XLA Ops:
  7.2 162.2 %all-reduce.2.cloned.1.call-start = ((), (), s32[]{:S(2)}) async-start(), calls=%async_computation.1 | async-start | bytes 6553600 | tf_op jit(solution)/shard_map/psum | solution.py:9
  240.9 6.7 copy-start
  240.9 6.7 copy-start.1
  240.9 600.4 %all-to-all-start = ((bf16[4,6400,512]{2,0,1:T(4,128)(2,1)}), bf16[4,6400,512]{2,0,1:T(4,128)(2,1)}, u32[]{:S(2)}, u32[]{:S(2)}) async-start(bf16[4,6400,512]{2,0,1:T(4,128)(2,1)} %copy.18), calls=%async_computation | async-start | bytes 52428800 | tf_op jit(solution)/shard_map/all_to_all | solution.py:12
Sparse Core Ops, SparseCore 0:
  33.9 135.4 all-reduce.1
where the time goes:
time: 907 us; the launch traced here: 906 us
  blocking collectives  590 us (65%)
  waiting for transfers between devices  136 us (15%)
  local copies, waits for them, and re-layouts  100 us (11%)
  other arithmetic  58.5 us (6%)
  between operations  14.1 us (2%)
    all_gather x1, blocking collectives, per_device(): row_router = lax.all_gather(part_router, 'shard', axis=0, tiled=True)  585 us
    psum x1, waiting for transfers between devices, per_device(): total_down = lax.psum(jnp.sum(latest_down * latest_down, axis=2), 'shard')  136 us
    all_to_all x2, local copies, waits for them, and re-layouts, per_device(): lax.all_to_all(narrow_down, 'shard', split_axis=1, concat_axis=2, tiled=T...  57.4 us
    convert_element_type x1, other arithmetic, per_device(): (latest_down / jnp.expand_dims(scale_down, 2)).astype(jnp.bfloat16)  34.3 us
    convert_element_type x1, local copies, waits for them, and re-layouts, per_device(): (latest_down / jnp.expand_dims(scale_down, 2)).astype(jnp.bfloat16)  33.4 us
    reduce_sum x1, other arithmetic, per_device(): total_down = lax.psum(jnp.sum(latest_down * latest_down, axis=2), 'shard')  24.2 us
  transfers between devices with their start and end apart: 2, of which 1 were waited for; matrix products, arithmetic and copies ran while one was open for 0% of the time, Pallas kernels for 0%

commit v1 on v0

v1 whole, which is shorter than its diff:
```python
import functools

import jax
import jax.numpy as jnp
from jax import lax
from jax.experimental import pallas as pl
from jax.experimental.pallas import tpu as pltpu
from jax.sharding import PartitionSpec as P


def partner(me, k, n):
    other, bit = me, 1
    while bit < n:
        if k & bit:
            other = other + bit * (1 - 2 * (lax.div(me, bit) % 2))
        bit *= 2
    return other


def exchange_kernel(n, narrow_ref, out_ref, send_sem, recv_sem, own_sem):
    me = lax.axis_index("shard")
    rows, width = out_ref.shape[1], narrow_ref.shape[2]
    partners = [partner(me, k, n) for k in range(1, n)]

    barrier = pltpu.get_barrier_semaphore()
    for other in partners:
        pl.semaphore_signal(
            barrier, inc=1, device_id={"shard": other}, device_id_type=pl.DeviceIdType.MESH
        )
    pl.semaphore_wait(barrier, n - 1)

    columns = pl.ds(pl.multiple_of(me * width, 128), width)

    def rows_of(device):
        return pl.ds(pl.multiple_of(device * rows, 16), rows)

    copies = []
    for k, other in enumerate(partners):
        copy = pltpu.make_async_remote_copy(
            src_ref=narrow_ref.at[:, rows_of(other), :],
            dst_ref=out_ref.at[:, :, columns],
            send_sem=send_sem.at[k],
            recv_sem=recv_sem.at[k],
            device_id={"shard": other},
            device_id_type=pl.DeviceIdType.MESH,
        )
        copy.start()
        copies.append(copy)
    own = pltpu.make_async_copy(
        narrow_ref.at[:, rows_of(me), :], out_ref.at[:, :, columns], own_sem
    )
    own.start()
    own.wait()
    for copy in copies:
        copy.wait()


def exchange(narrow_down, n):
    experts, inner, width = narrow_down.shape
    return pl.pallas_call(
        functools.partial(exchange_kernel, n),
        out_shape=jax.ShapeDtypeStruct((experts, inner // n, width * n), narrow_down.dtype),
        in_specs=[pl.BlockSpec(memory_space=pl.ANY)],
        out_specs=pl.BlockSpec(memory_space=pl.ANY),
        scratch_shapes=[
            pltpu.SemaphoreType.DMA((n - 1,)),
            pltpu.SemaphoreType.DMA((n - 1,)),
            pltpu.SemaphoreType.DMA,
        ],
        compiler_params=pltpu.CompilerParams(collective_id=0, has_side_effects=True),
        name="exchange",
    )(narrow_down)


def per_device(n, train_down, other_down, router_weight, router_gain):
    latest_down = train_down + other_down.astype(jnp.float32)
    part_down = jnp.sum(latest_down * latest_down, axis=2)
    total_down = jnp.sum(lax.all_gather(part_down, "shard", axis=0), axis=0)
    scale_down = jnp.sqrt(total_down)
    narrow_down = (latest_down / jnp.expand_dims(scale_down, 2)).astype(jnp.bfloat16)
    ready_down = exchange(narrow_down, n)
    scale_down = lax.dynamic_slice_in_dim(
        scale_down, lax.axis_index("shard") * ready_down.shape[1], ready_down.shape[1], axis=1
    )
    part_router = (router_weight * router_gain[:, None]).astype(jnp.bfloat16)
    row_router = lax.all_gather(part_router, "shard", axis=0, tiled=True)
    serve_router = lax.all_gather(row_router, "expert", axis=1, tiled=True)
    return (ready_down, scale_down, serve_router)


def solution(mesh):
    in_specs = (
        P("expert", None, "shard"),
        P("expert", None, "shard"),
        P("shard", "expert"),
        P("shard"),
    )
    out_specs = (P("expert", "shard", None), P("expert", "shard"), P())
    return jax.shard_map(
        functools.partial(per_device, mesh.shape["shard"]),
        mesh=mesh,
        in_specs=in_specs,
        out_specs=out_specs,
        check_vma=False,
    )
```

time: 907 us -> 708 us (0.78)
  Pallas kernels: 0 us -> 428 us
  blocking collectives: 590 us -> 201 us
  waiting for transfers between devices: 136 us -> 0 us
  local copies, waits for them, and re-layouts: 100 us -> 19.4 us
  between operations: 14.1 us -> 0.69 us
    pallas_call x0 -> x1, Pallas kernels: none -> 428 us  [exchange(): pl.pallas_call(functools.partial(exchange_kernel, n), out_shape=jax.Shape...]
    all_gather x1, blocking collectives: 585 us -> 162 us  [per_device(): row_router = lax.all_gather(part_router, 'shard', axis=0, tiled=True)]
    psum x1 -> x0, waiting for transfers between devices: 136 us -> none  [per_device(): total_down = lax.psum(jnp.sum(latest_down * latest_down, axis=2), 'shard')]
    all_to_all x2 -> x0, local copies, waits for them, and re-layouts: 57.4 us -> none  [per_device(): lax.all_to_all(narrow_down, 'shard', split_axis=1, concat_axis=2, tiled=T...]
    all_gather x0 -> x1, blocking collectives: none -> 33.9 us  [per_device(): total_down = jnp.sum(lax.all_gather(part_down, 'shard', axis=0), axis=0)]
    convert_element_type x1 -> x0, local copies, waits for them, and re-layouts: 33.4 us -> none  [per_device(): (latest_down / jnp.expand_dims(scale_down, 2)).astype(jnp.bfloat16)]
    unnamed x7 -> x6, local copies, waits for them, and re-layouts: 4.74 us -> 18.6 us
    reduce_sum x1 -> x2, other arithmetic: 24.2 us -> 24.4 us  [the longest x1 24.2 us: per_device(): part_down = jnp.sum(latest_down * latest_down, axis=2)]
  transfers between devices with their start and end apart: 2 -> 0, of which waited for: 1 -> 0; matrix products, arithmetic and copies ran while one was open for 0% -> 0% of each run, Pallas kernels for 0% -> 0%
where the time goes in v1:
time: 708 us
  Pallas kernels  428 us (60%)
  blocking collectives  201 us (28%)
  other arithmetic  58.6 us (8%)
  local copies, waits for them, and re-layouts  19.4 us (3%)
    pallas_call x1, Pallas kernels, exchange(): pl.pallas_call(functools.partial(exchange_kernel, n), out_shape=jax.Shape...  428 us
    all_gather x1, blocking collectives, per_device(): row_router = lax.all_gather(part_router, 'shard', axis=0, tiled=True)  162 us
    convert_element_type x1, other arithmetic, per_device(): (latest_down / jnp.expand_dims(scale_down, 2)).astype(jnp.bfloat16)  34.3 us
    all_gather x1, blocking collectives, per_device(): total_down = jnp.sum(lax.all_gather(part_down, 'shard', axis=0), axis=0)  33.9 us
    reduce_sum x1, other arithmetic, per_device(): part_down = jnp.sum(latest_down * latest_down, axis=2)  24.2 us
    unnamed x6, local copies, waits for them, and re-layouts  18.6 us

profile of v1, /device:TPU:0, one launch (start us, length us, event | category | flops | bytes accessed | tf_op | source)
XLA Modules:
  0.0 707.8 jit_solution(1934832086001310032)
XLA Ops:
  0.6 24.2 %multiply_reduce_fusion = f32[4,6400]{1,0:T(4,128)S(1)} fusion(f32[4,6400,512]{2,1,0:T(8,128)} %param.4, bf16[4,6400,512]{2,1,0:T(8,128)(2,1)} %param.5), kind=kLoop, calls=%fused_computation.1 | loop fusion | flops 52403200 | bytes 78745600 | tf_op jit(solution)/shard_map/reduce_sum | solution.py:77
  24.9 33.9 %all-gather.1 = f32[8,4,6400]{2,1,0:T(4,128)S(1)} all-gather(f32[1,4,6400]{2,1,0:T(4,128)S(1)} %bitcast.5), channel_id=2, replica_groups=mesh['expert'=4,'shard'=8] {'shard'}, dimensions={0}, use_global_device_ids=true | all-gather | bytes 921600 | tf_op jit(solution)/shard_map/all_gather | solution.py:78
  58.8 0.1 reduce_sum.19
  58.9 0.1 sqrt.7
  59.0 0.7 constant_dynamic-slice_fusion
  59.7 34.3 %divide_convert_fusion.narrow_ref = bf16[4,6400,512]{2,1,0:T(8,128)(2,1)} fusion(f32[4,6400,512]{2,1,0:T(8,128)} %param.4, bf16[4,6400,512]{2,1,0:T(8,128)(2,1)} %param.5, f32[4,6400]{1,0:T(4,128)S(1)} %sqrt.7), kind=kLoop, calls=%fused_computation | loop fusion | flops 52428800 | bytes 104960000 | tf_op jit(solution)/shard_map/convert_element_type | solution.py:80
  93.9 0.0 copy-start
  93.9 0.0 copy-start.1
  93.9 428.1 %exchange.1 = bf16[4,800,4096]{2,1,0:T(8,128)(2,1)} custom-call(bf16[4,6400,512]{2,1,0:T(8,128)(2,1)} %divide_convert_fusion.narrow_ref), custom_call_target="tpu_custom_call" | custom-call | tf_op jit(solution)/shard_map/exchange/pallas_call | solution.py:60
  522.1 0.0 copy-done
  522.1 0.0 copy-done.1
  522.1 161.6 %all_gather.14 = bf16[4096,4]{0,1:T(4,128)(2,1)S(1)} all-gather(bf16[512,4]{0,1:T(4,128)(2,1)S(1)} %multiply_convert_fusion), channel_id=1, replica_groups=mesh['expert'=4,'shard'=8] {'shard'}, dimensions={0}, use_global_device_ids=true | all-gather | bytes 36864 | tf_op jit(solution)/shard_map/all_gather | solution.py:86
  683.7 5.4 all-gather.2
  689.1 0.7 reshape.14
  689.8 17.9 %copy.8 = bf16[4,800,4096]{2,1,0:T(8,128)(2,1)} copy(bf16[4,800,4096]{2,1,0:T(8,128)(2,1)} %exchange.1) | data formatting | bytes 52428800
  (1 shorter events, 0.0 us)
Async XLA Ops:
  93.9 428.1 %copy-start = (f32[512,4]{0,1:T(4,128)S(1)}, f32[512,4]{0,1:T(4,128)}, u32[]{:S(2)}) copy-start(f32[512,4]{0,1:T(4,128)} %param.6) | copy-start | bytes 24580
  93.9 428.2 %copy-start.1 = (f32[512]{0:T(512)S(1)}, f32[512]{0:T(512)}, u32[]{:S(2)}) copy-start(f32[512]{0:T(512)} %param.7) | copy-start | bytes 6148
